TPU v7x, 32 devices: a whole 2x2x4 slice. The times are simulated.
32 devices in a mesh: seq: 8 (over z, x), res: 4 (over y, core).
Axes of the slice: x: 2, y: 2, z: 4, core: 2. Of those that a mesh axis runs over, the one named last changes fastest.
Arguments:
- alignment: bfloat16 [128, 4, 128, 256], P('seq', 'res'), may hold values from -8 to 8
- gain_attn: float32 [256], replicated, may hold values from 0.1 to 1.9
- w_proj: bfloat16 [256, 4, 256], replicated, may hold values from -0.75 to 0.75
- w_out: bfloat16 [256, 256], replicated, may hold values from -0.375 to 0.375
- gain_head: float32 [256], replicated, may hold values from 0.1 to 1.9
- w_head: bfloat16 [256, 23], replicated, may hold values from -1 to 1
- masked: int32 [128, 4, 128], P('res', None, 'seq'), may hold values from 0 to 1
- labels: int32 [128, 4, 128], P('res', None, 'seq'), may hold values from 0 to 22
Outputs:
- updated: bfloat16 [128, 4, 128, 256], P('res', None, 'seq')
- masked_loss: float32 [], replicated
- mask_share: float32 [], replicated
All inputs are finite; a program needn't handle non-finite values.
Results may differ from a plain program's by a relative error of at most 0.011.
Values may be sent and summed in bfloat16 or wider, within the bound.
A program may use at most 192 MiB of HBM per device.

v0:
```python
import jax
import jax.numpy as jnp
from jax import lax
from jax.sharding import PartitionSpec as P

HEADS = 8
HEAD_DIM = 32


def normalize(values, gain):
    mean = jnp.mean(values, axis=-1, keepdims=True)
    centred = values - mean
    spread = jnp.mean(centred * centred, axis=-1, keepdims=True)
    return centred * lax.rsqrt(spread + 1e-05) * gain


def project(flat_rows, gain_attn, w_proj):
    features = flat_rows.shape[1]
    normed = normalize(flat_rows.astype(jnp.float32), gain_attn).astype(jnp.bfloat16)
    return jnp.dot(
        normed, w_proj.reshape(features, 4 * features), preferred_element_type=jnp.float32
    ).astype(jnp.bfloat16)


def column_attention(queries, key_part, value_part):
    inv_root = HEAD_DIM ** (-0.5)
    scores = (
        jnp.einsum("shd,thd->hst", queries, key_part, preferred_element_type=jnp.float32) * inv_root
    )
    probs = jnp.exp(scores)
    totals = jnp.sum(probs, axis=2)
    weighted = jnp.einsum(
        "hst,thd->shd", probs.astype(jnp.bfloat16), value_part, preferred_element_type=jnp.float32
    )
    return (weighted, totals)


def finish(flat_rows, gated, w_out):
    summed = flat_rows.astype(jnp.float32) + jnp.dot(
        gated, w_out, preferred_element_type=jnp.float32
    )
    return summed.astype(jnp.bfloat16)


def on_device(alignment, gain_attn, w_proj, w_out, gain_head, w_head, masked, labels):
    weights = masked.reshape(-1).astype(jnp.float32)
    local_count = jnp.sum(weights)
    local_rows, single_block, segment, features = alignment.shape
    seq_devices = lax.axis_size("seq")
    split_view = alignment.reshape(local_rows, seq_devices, segment // seq_devices, features)
    column_block = lax.all_to_all(split_view, "seq", split_axis=1, concat_axis=0, tiled=True)
    seq_total, single, col_count, features = column_block.shape
    by_column = jnp.transpose(column_block.reshape(seq_total, col_count, features), (1, 0, 2))
    flat_rows = by_column.reshape(col_count * seq_total, features)
    projected = project(flat_rows, gain_attn, w_proj).reshape(
        col_count, seq_total, 4, HEADS, HEAD_DIM
    )

    def per_column(picked):
        weighted, totals = column_attention(picked[:, 0], picked[:, 1], picked[:, 2])
        attended = weighted / totals.T[:, :, None]
        gated_col = attended * jax.nn.sigmoid(picked[:, 3].astype(jnp.float32))
        return gated_col.reshape(seq_total, features).astype(jnp.bfloat16)

    gated = lax.map(per_column, projected).reshape(col_count * seq_total, features)
    result = finish(flat_rows, gated, w_out).reshape(col_count, seq_total, features)
    result = jnp.transpose(result, (1, 0, 2)).reshape(seq_total, single, col_count, features)
    updated = lax.all_to_all(result, "res", split_axis=0, concat_axis=1, tiled=True)
    features = updated.shape[3]
    flat_out = updated.reshape(-1, features)
    head_in = normalize(flat_out.astype(jnp.float32), gain_head).astype(jnp.bfloat16)
    logits = jnp.einsum("rc,ck->kr", head_in, w_head, preferred_element_type=jnp.float32)
    log_total = jnp.log(jnp.sum(jnp.exp(logits), axis=0))
    classes = jnp.arange(logits.shape[0], dtype=jnp.int32)[:, None]
    picked = jnp.sum(jnp.where(classes == labels.reshape(1, -1), logits, 0.0), axis=0)
    errors = log_total - picked
    local_loss = jnp.sum(errors * weights)
    loss_sum, mask_count = lax.psum((local_loss, local_count), ("seq", "res"))
    entries = flat_out.shape[0] * lax.axis_size("seq") * lax.axis_size("res")
    masked_loss = loss_sum / (1.0 + mask_count)
    mask_share = mask_count / entries
    return (updated, masked_loss, mask_share)


def solution(mesh):
    in_specs = (
        P("seq", "res", None, None),
        P(),
        P(),
        P(),
        P(),
        P(),
        P("res", None, "seq"),
        P("res", None, "seq"),
    )
    out_specs = (P("res", None, "seq", None), P(), P())
    return jax.shard_map(
        on_device, mesh=mesh, in_specs=in_specs, out_specs=out_specs, check_vma=False
    )
```

profile of v0, /device:TPU:12, one launch (start us, length us, event | category | flops | bytes accessed | tf_op | source)
XLA Modules:
  0.0 152.1 jit_solution(10787070603162363327)
XLA Ops:
  0.7 2.4 %copy.61 = bf16[16,8,16,256]{3,2,0,1:T(8,128)(2,1)} copy(bf16[16,8,16,256]{3,2,1,0:T(8,128)(2,1)} %bitcast.113) | data formatting | bytes 2097152 | tf_op jit(solution)/shard_map/reshape | solution.py:50
  3.0 6.3 %all-to-all-start = ((bf16[16,8,16,256]{3,2,0,1:T(8,128)(2,1)}), bf16[16,8,16,256]{3,2,0,1:T(8,128)(2,1)S(1)}, u32[]{:S(2)}, u32[]{:S(2)}) async-start(bf16[16,8,16,256]{3,2,0,1:T(8,128)(2,1)} %copy.61), calls=%async_computation | async-start | bytes 2097152 | tf_op jit(solution)/shard_map/all_to_all | solution.py:51
  9.4 23.3 %all-to-all-done = bf16[16,8,16,256]{3,2,0,1:T(8,128)(2,1)S(1)} async-done(((bf16[16,8,16,256]{3,2,0,1:T(8,128)(2,1)}), bf16[16,8,16,256]{3,2,0,1:T(8,128)(2,1)S(1)}, u32[]{:S(2)}, u32[]{:S(2)}) %all-to-all-start) | async-done | bytes 1048608 | tf_op jit(solution)/shard_map/all_to_all | solution.py:51
  32.9 1.2 bitcast_reduce_fusion
  34.1 1.2 copy.62
  35.3 1.6 %multiply_reduce_fusion.1 = f32[16,128]{1,0:T(8,128)S(1)} fusion(f32[16,128]{1,0:T(8,128)S(1)} %broadcast_multiply_fusion.1, f32[128,16,256]{2,1,0:T(8,128)S(1)} %bitcast.100), kind=kLoop, calls=%fused_computation.24 | loop fusion | flops 1570816 | bytes 2113536 | tf_op jit(solution)/shard_map/reduce_sum | solution.py:13
  37.0 1.4 multiply_convert_fusion
  38.3 3.2 %convolution_convert_fusion = bf16[2048,1024]{1,0:T(8,128)(2,1)} fusion(bf16[2048,256]{1,0:T(8,128)(2,1)S(1)} %bitcast.109, bf16[256,1024]{1,0:T(8,128)(2,1)S(1)} %bitcast.111), kind=kOutput, calls=%fused_computation.12 | convolution fusion | flops 1075838976 | bytes 5767168 | tf_op jit(solution)/shard_map/dot_general | solution.py:20
  41.5 6.5 %copy.63 = bf16[2048,1024]{0,1:T(8,128)(2,1)} copy(bf16[2048,1024]{1,0:T(8,128)(2,1)} %convolution_convert_fusion) | data formatting | bytes 8388608 | tf_op jit(solution)/shard_map/convert_element_type | solution.py:22
  48.0 3.6 %copy.80 = bf16[128,8,16,128]{3,2,1,0:T(8,128)(2,1)S(1)} copy(bf16[128,8,16,128]{3,1,2,0:T(8,128)(2,1)} %bitcast.106) | data formatting | bytes 8388608
  51.6 3.0 %copy.64 = bf16[16,128,4,8,32]{1,4,3,2,0:T(8,128)(2,1)} copy(bf16[16,128,4,8,32]{1,0,4,3,2:T(8,128)(2,1)S(1)} %bitcast.107) | data formatting | bytes 8388608 | tf_op jit(solution)/shard_map/while | solution.py:65
  54.7 26.1 %while.10 = (s32[]{:T(128)}, bf16[16,128,256]{2,1,0:T(8,128)(2,1)S(1)}, bf16[16,128,4,8,32]{1,4,3,2,0:T(8,128)(2,1)}, s32[]{:T(128)}) while((s32[]{:T(128)}, bf16[16,128,256]{2,1,0:T(8,128)(2,1)S(1)}, bf16[16,128,4,8,32]{1,4,3,2,0:T(8,128)(2,1)}, s32[]{:T(128)}) %tuple.42), condition=%wide.region_4.0_spmd, body=%wide.region_2.4_spmd.sunk | while | flops 17398784 | bytes 1646653 | solution.py:65
  56.3 1.0 dynamic-slice_bitcast_fusion.2
  57.9 1.0 dynamic-slice_bitcast_fusion.2
  59.6 1.0 dynamic-slice_bitcast_fusion.2
  61.2 1.0 dynamic-slice_bitcast_fusion.2
  62.8 1.0 dynamic-slice_bitcast_fusion.2
  64.5 1.0 dynamic-slice_bitcast_fusion.2
  66.1 1.0 dynamic-slice_bitcast_fusion.2
  67.7 1.0 dynamic-slice_bitcast_fusion.2
  69.4 1.0 dynamic-slice_bitcast_fusion.2
  71.0 1.0 dynamic-slice_bitcast_fusion.2
  72.6 1.0 dynamic-slice_bitcast_fusion.2
  74.3 1.0 dynamic-slice_bitcast_fusion.2
  75.9 1.0 dynamic-slice_bitcast_fusion.2
  77.5 1.0 dynamic-slice_bitcast_fusion.2
  81.3 1.6 %copy.85 = bf16[16,128,256]{2,0,1:T(8,128)(2,1)} copy(bf16[16,128,256]{2,1,0:T(8,128)(2,1)S(1)} %bitcast.110) | data formatting | bytes 2097152 | tf_op jit(solution)/shard_map/reshape | solution.py:66
  82.8 4.0 %all-to-all-start.1 = ((bf16[128,1,16,256]{3,2,1,0:T(8,128)(2,1)}), bf16[128,1,16,256]{3,2,1,0:T(8,128)(2,1)S(1)}, u32[]{:S(2)}, u32[]{:S(2)}) async-start(bf16[128,1,16,256]{3,2,1,0:T(8,128)(2,1)} %bitcast.79), calls=%async_computation.1 | async-start | bytes 2097152 | tf_op jit(solution)/shard_map/all_to_all | solution.py:68
  87.1 12.5 %all-to-all-done.1 = bf16[128,1,16,256]{3,2,1,0:T(8,128)(2,1)S(1)} async-done(((bf16[128,1,16,256]{3,2,1,0:T(8,128)(2,1)}), bf16[128,1,16,256]{3,2,1,0:T(8,128)(2,1)S(1)}, u32[]{:S(2)}, u32[]{:S(2)}) %all-to-all-start.1) | async-done | bytes 1048608 | tf_op jit(solution)/shard_map/all_to_all | solution.py:68
  102.5 1.1 exponential_reduce_fusion
  104.4 42.4 %all-reduce = (f32[]{:T(128)}, f32[]{:T(128)}) all-reduce(f32[]{:T(128)} %get-tuple-element.57, f32[]{:T(128)} %get-tuple-element.56), channel_id=1, replica_groups=mesh['seq'=8,'res'=4] {'seq','res'}, use_global_device_ids=true, to_apply=%region_10.11 | all-reduce | flops 2 | bytes 16 | tf_op jit(solution)/shard_map/psum | solution.py:78
  148.1 1.1 copy.75
  (105 shorter events, 16.6 us)
Async XLA Ops:
  0.6 80.2 %copy-start = (bf16[256,256]{1,0:T(8,128)(2,1)S(1)}, bf16[256,256]{1,0:T(8,128)(2,1)}, u32[]{:S(2)}) copy-start(bf16[256,256]{1,0:T(8,128)(2,1)} %param.13) | copy-start | bytes 393220
  0.6 8.6 %copy-start.2 = (bf16[256,4,256]{2,1,0:T(4,128)(2,1)S(1)}, bf16[256,4,256]{2,1,0:T(4,128)(2,1)}, u32[]{:S(2)}) copy-start(bf16[256,4,256]{2,1,0:T(4,128)(2,1)} %param.12) | copy-start | bytes 1572868
  3.0 29.6 %all-to-all-start = ((bf16[16,8,16,256]{3,2,0,1:T(8,128)(2,1)}), bf16[16,8,16,256]{3,2,0,1:T(8,128)(2,1)S(1)}, u32[]{:S(2)}, u32[]{:S(2)}) async-start(bf16[16,8,16,256]{3,2,0,1:T(8,128)(2,1)} %copy.61), calls=%async_computation | async-start | bytes 2097152 | tf_op jit(solution)/shard_map/all_to_all | solution.py:51
  35.3 1.7 %copy-start.5 = (f32[256]{0:T(256)S(1)}, f32[256]{0:T(256)}, u32[]{:S(2)}) copy-start(f32[256]{0:T(256)} %param.11) | copy-start | bytes 3076
  51.6 3.0 %copy-start.1 = (bf16[16,128,256]{2,1,0:T(8,128)(2,1)S(1)}, bf16[16,128,256]{2,1,0:T(8,128)(2,1)}, u32[]{:S(2)}) copy-start(bf16[16,128,256]{2,1,0:T(8,128)(2,1)} %custom-call) | copy-start | bytes 3145732
  81.3 5.6 %copy-start.3 = (s32[32,4,16]{0,2,1:T(8,128)S(1)}, s32[32,4,16]{0,2,1:T(8,128)}, u32[]{:S(2)}) copy-start(s32[32,4,16]{0,2,1:T(8,128)} %param.17) | copy-start | bytes 24580
  81.3 5.7 %copy-start.4 = (s32[32,4,16]{0,2,1:T(8,128)S(1)}, s32[32,4,16]{0,2,1:T(8,128)}, u32[]{:S(2)}) copy-start(s32[32,4,16]{0,2,1:T(8,128)} %param.16) | copy-start | bytes 24580
  82.8 16.8 %all-to-all-start.1 = ((bf16[128,1,16,256]{3,2,1,0:T(8,128)(2,1)}), bf16[128,1,16,256]{3,2,1,0:T(8,128)(2,1)S(1)}, u32[]{:S(2)}, u32[]{:S(2)}) async-start(bf16[128,1,16,256]{3,2,1,0:T(8,128)(2,1)} %bitcast.79), calls=%async_computation.1 | async-start | bytes 2097152 | tf_op jit(solution)/shard_map/all_to_all | solution.py:68
  100.2 1.4 copy-start.6
where the time goes:
time: 153 us; the launch traced here: 152 us
  blocking collectives  42.4 us (28%)
  local copies, waits for them, and re-layouts  38.2 us (25%)
  waiting for transfers between devices  35.8 us (23%)
  matrix products  12.7 us (8%)
  starting transfers between devices  10.2 us (7%)
  other arithmetic  7 us (5%)
  between operations  5.09 us (3%)
    psum x1, blocking collectives, on_device(): loss_sum, mask_count = lax.psum((local_loss, local_count), ('seq', 'res'))  42.4 us
    all_to_all x1, waiting for transfers between devices, on_device(): lax.all_to_all(split_view, 'seq', split_axis=1, concat_axis=0, tiled=True)  23.3 us
    squeeze x16, local copies, waits for them, and re-layouts, on_device(): lax.map(per_column, projected).reshape(col_count * seq_total, features)  15.5 us
    all_to_all x1, waiting for transfers between devices, on_device(): lax.all_to_all(result, 'res', split_axis=0, concat_axis=1, tiled=True)  12.5 us
    convert_element_type x1, local copies, waits for them, and re-layouts, project(): return jnp.dot(normed, w_proj.reshape(features, 4 * features), preferred_...  6.52 us
    all_to_all x1, starting transfers between devices, on_device(): lax.all_to_all(split_view, 'seq', split_axis=1, concat_axis=0, tiled=True)  6.25 us
    dot_general x16, matrix products, column_attention(): jnp.einsum('shd,thd->hst', queries, key_part, preferred_element_type=jnp....  5.03 us
    unnamed x19, local copies, waits for them, and re-layouts  4.99 us
  transfers between devices with their start and end apart: 2, of which 2 were waited for; matrix products, arithmetic and copies ran while one was open for 0% of the time, Pallas kernels for 0%

commit v1 on v0

--- a/solution.py
+++ b/solution.py
@@ -48,7 +48,15 @@
     local_rows, single_block, segment, features = alignment.shape
     seq_devices = lax.axis_size("seq")
     split_view = alignment.reshape(local_rows, seq_devices, segment // seq_devices, features)
-    column_block = lax.all_to_all(split_view, "seq", split_axis=1, concat_axis=0, tiled=True)
+    ways, here = (lax.axis_size("seq"), lax.axis_index("seq"))
+    width = split_view.shape[1] // ways
+    turned = jnp.roll(split_view, -here * width, axis=1)
+    got = [lax.slice_in_dim(turned, 0, width, axis=1)]
+    for far in range(1, ways):
+        sent = lax.slice_in_dim(turned, far * width, (far + 1) * width, axis=1)
+        got.append(lax.ppermute(sent, "seq", [(d, (d + far) % ways) for d in range(ways)]))
+    line = jnp.concatenate(got[::-1], axis=0)
+    column_block = jnp.roll(line, (here + 1) * got[0].shape[0], axis=0)
     seq_total, single, col_count, features = column_block.shape
     by_column = jnp.transpose(column_block.reshape(seq_total, col_count, features), (1, 0, 2))
     flat_rows = by_column.reshape(col_count * seq_total, features)

time: 153 us -> 148 us (0.967)
  waiting for transfers between devices: 35.8 us -> 29 us
  starting transfers between devices: 10.2 us -> 13.9 us
  other arithmetic: 7 us -> 4.89 us
    all_to_all x1 -> x0, waiting for transfers between devices: 23.3 us -> none  [on_device(): lax.all_to_all(split_view, 'seq', split_axis=1, concat_axis=0, tiled=True)]
    ppermute x0 -> x7, waiting for transfers between devices: none -> 17.1 us  [on_device(): lax.ppermute(sent, 'seq', [(d, (d + far) % ways) for d in range(ways)])]
    ppermute x0 -> x7, starting transfers between devices: none -> 9.87 us  [on_device(): lax.ppermute(sent, 'seq', [(d, (d + far) % ways) for d in range(ways)])]
    all_to_all x1 -> x0, starting transfers between devices: 6.25 us -> none  [on_device(): lax.all_to_all(split_view, 'seq', split_axis=1, concat_axis=0, tiled=True)]
    unnamed x19 -> x38, local copies, waits for them, and re-layouts: 4.99 us -> 5.78 us
  transfers between devices with their start and end apart: 2 -> 8, of which waited for: 2 -> 6; matrix products, arithmetic and copies ran while one was open for 0% -> 1% of each run, Pallas kernels for 0% -> 0%
where the time goes in v1:
time: 148 us; the launch traced here: 146 us
  blocking collectives  41.9 us (28%)
  local copies, waits for them, and re-layouts  38.1 us (26%)
  waiting for transfers between devices  29 us (20%)
  starting transfers between devices  13.9 us (9%)
  matrix products  12 us (8%)
  between operations  5.29 us (4%)
  other arithmetic  4.89 us (3%)
    psum x1, blocking collectives, on_device(): loss_sum, mask_count = lax.psum((local_loss, local_count), ('seq', 'res'))  41.9 us
    ppermute x7, waiting for transfers between devices, on_device(): lax.ppermute(sent, 'seq', [(d, (d + far) % ways) for d in range(ways)])  17.1 us
    squeeze x16, local copies, waits for them, and re-layouts, on_device(): lax.map(per_column, projected).reshape(col_count * seq_total, features)  15.5 us
    all_to_all x1, waiting for transfers between devices, on_device(): lax.all_to_all(result, 'res', split_axis=0, concat_axis=1, tiled=True)  11.9 us
    ppermute x7, starting transfers between devices, on_device(): lax.ppermute(sent, 'seq', [(d, (d + far) % ways) for d in range(ways)])  9.87 us
    convert_element_type x1, local copies, waits for them, and re-layouts, project(): return jnp.dot(normed, w_proj.reshape(features, 4 * features), preferred_...  6.52 us
    unnamed x38, local copies, waits for them, and re-layouts  5.78 us
    dot_general x16, matrix products, column_attention(): jnp.einsum('shd,thd->hst', queries, key_part, preferred_element_type=jnp....  5.03 us
  transfers between devices with their start and end apart: 8, of which 6 were waited for; matrix products, arithmetic and copies ran while one was open for 1% of the time, Pallas kernels for 0%

profile of v1, /device:TPU:12, one launch (start us, length us, event | category | flops | bytes accessed | tf_op | source)
XLA Modules:
  0.0 145.7 jit_solution(7844516990078141470)
XLA Ops:
  0.7 1.8 %copy.52 = bf16[16,8,16,256]{3,0,2,1:T(8,128)(2,1)S(1)} copy(bf16[16,8,16,256]{3,2,1,0:T(8,128)(2,1)} %bitcast.109) | data formatting | bytes 2097152 | tf_op jit(solution)/shard_map/reshape | solution.py:50
  3.7 1.4 collective-permute-start
  5.1 3.6 %collective-permute-start.1 = (bf16[16,1,16,256]{3,0,2,1:T(8,128)(2,1)S(1)}, bf16[16,1,16,256]{3,0,2,1:T(8,128)(2,1)S(1)}, u32[]{:S(2)}, u32[]{:S(2)}) collective-permute-start(bf16[16,1,16,256]{3,0,2,1:T(8,128)(2,1)S(1)} %get-tuple-element.67), channel_id=1, source_target_pairs={{0,24},{4,28},{8,0},{12,4},{16,8},{20,12},{24,16},{28,20},{1,25},{... | collective-permute-start | bytes 393224 | tf_op jit(solution)/shard_map/ppermute | solution.py:57
  8.7 3.3 %collective-permute-start.4 = (bf16[16,1,16,256]{3,0,2,1:T(8,128)(2,1)S(1)}, bf16[16,1,16,256]{3,0,2,1:T(8,128)(2,1)S(1)}, u32[]{:S(2)}, u32[]{:S(2)}) collective-permute-start(bf16[16,1,16,256]{3,0,2,1:T(8,128)(2,1)S(1)} %get-tuple-element.64), channel_id=1, source_target_pairs={{0,12},{4,16},{8,20},{12,24},{16,28},{20,0},{24,4},{28,8},{1,13},{... | collective-permute-start | bytes 393224 | tf_op jit(solution)/shard_map/ppermute | solution.py:57
  12.1 1.6 %collective-permute-start.5 = (bf16[16,1,16,256]{3,0,2,1:T(8,128)(2,1)S(1)}, bf16[16,1,16,256]{3,0,2,1:T(8,128)(2,1)S(1)}, u32[]{:S(2)}, u32[]{:S(2)}) collective-permute-start(bf16[16,1,16,256]{3,0,2,1:T(8,128)(2,1)S(1)} %get-tuple-element.63), channel_id=1, source_target_pairs={{0,8},{4,12},{8,16},{12,20},{16,24},{20,28},{24,0},{28,4},{1,9},{5... | collective-permute-start | bytes 393224 | tf_op jit(solution)/shard_map/ppermute | solution.py:57
  13.7 11.3 %collective-permute-done.1 = bf16[16,1,16,256]{3,0,2,1:T(8,128)(2,1)S(1)} collective-permute-done((bf16[16,1,16,256]{3,0,2,1:T(8,128)(2,1)S(1)}, bf16[16,1,16,256]{3,0,2,1:T(8,128)(2,1)S(1)}, u32[]{:S(2)}, u32[]{:S(2)}) %collective-permute-start.1) | collective-permute-done | bytes 131104 | tf_op jit(solution)/shard_map/ppermute | solution.py:57
  25.1 2.0 %collective-permute-done.2 = bf16[16,1,16,256]{3,0,2,1:T(8,128)(2,1)S(1)} collective-permute-done((bf16[16,1,16,256]{3,0,2,1:T(8,128)(2,1)}, bf16[16,1,16,256]{3,0,2,1:T(8,128)(2,1)S(1)}, u32[]{:S(2)}, u32[]{:S(2)}) %collective-permute-start.2) | collective-permute-done | bytes 131104 | tf_op jit(solution)/shard_map/ppermute | solution.py:57
  27.9 2.7 %collective-permute-done.5 = bf16[16,1,16,256]{3,0,2,1:T(8,128)(2,1)S(1)} collective-permute-done((bf16[16,1,16,256]{3,0,2,1:T(8,128)(2,1)S(1)}, bf16[16,1,16,256]{3,0,2,1:T(8,128)(2,1)S(1)}, u32[]{:S(2)}, u32[]{:S(2)}) %collective-permute-start.5) | collective-permute-done | bytes 131104 | tf_op jit(solution)/shard_map/ppermute | solution.py:57
  33.1 3.2 %convolution_convert_fusion = bf16[2048,1024]{1,0:T(8,128)(2,1)} fusion(bf16[2048,256]{1,0:T(8,128)(2,1)S(1)} %bitcast.105, bf16[256,1024]{1,0:T(8,128)(2,1)S(1)} %bitcast.107), kind=kOutput, calls=%fused_computation.12 | convolution fusion | flops 1075838976 | bytes 5767168 | tf_op jit(solution)/shard_map/dot_general | solution.py:20
  36.3 6.5 %copy.54 = bf16[2048,1024]{0,1:T(8,128)(2,1)} copy(bf16[2048,1024]{1,0:T(8,128)(2,1)} %convolution_convert_fusion) | data formatting | bytes 8388608 | tf_op jit(solution)/shard_map/convert_element_type | solution.py:22
  42.8 3.6 %copy.71 = bf16[128,8,16,128]{3,2,1,0:T(8,128)(2,1)S(1)} copy(bf16[128,8,16,128]{3,1,2,0:T(8,128)(2,1)} %bitcast.102) | data formatting | bytes 8388608
  46.4 3.0 %copy.55 = bf16[16,128,4,8,32]{1,4,3,2,0:T(8,128)(2,1)} copy(bf16[16,128,4,8,32]{1,0,4,3,2:T(8,128)(2,1)S(1)} %bitcast.103) | data formatting | bytes 8388608 | tf_op jit(solution)/shard_map/while | solution.py:73
  49.4 26.1 %while.10 = (s32[]{:T(128)}, bf16[16,128,256]{2,1,0:T(8,128)(2,1)S(1)}, bf16[16,128,4,8,32]{1,4,3,2,0:T(8,128)(2,1)}, s32[]{:T(128)}) while((s32[]{:T(128)}, bf16[16,128,256]{2,1,0:T(8,128)(2,1)S(1)}, bf16[16,128,4,8,32]{1,4,3,2,0:T(8,128)(2,1)}, s32[]{:T(128)}) %tuple.46), condition=%wide.region_4.5_spmd, body=%wide.region_2.4_spmd.sunk | while | flops 17398784 | bytes 1646653 | solution.py:73
  51.1 1.0 dynamic-slice_bitcast_fusion.2
  52.7 1.0 dynamic-slice_bitcast_fusion.2
  54.3 1.0 dynamic-slice_bitcast_fusion.2
  56.0 1.0 dynamic-slice_bitcast_fusion.2
  57.6 1.0 dynamic-slice_bitcast_fusion.2
  59.2 1.0 dynamic-slice_bitcast_fusion.2
  60.9 1.0 dynamic-slice_bitcast_fusion.2
  62.5 1.0 dynamic-slice_bitcast_fusion.2
  64.1 1.0 dynamic-slice_bitcast_fusion.2
  65.8 1.0 dynamic-slice_bitcast_fusion.2
  67.4 1.0 dynamic-slice_bitcast_fusion.2
  69.1 1.0 dynamic-slice_bitcast_fusion.2
  70.7 1.0 dynamic-slice_bitcast_fusion.2
  74.0 1.0 dynamic-slice_bitcast_fusion.2
  76.1 1.6 %copy.73 = bf16[16,128,256]{2,0,1:T(8,128)(2,1)} copy(bf16[16,128,256]{2,1,0:T(8,128)(2,1)S(1)} %bitcast.106) | data formatting | bytes 2097152 | tf_op jit(solution)/shard_map/reshape | solution.py:74
  77.6 4.0 %all-to-all-start = ((bf16[128,1,16,256]{3,2,1,0:T(8,128)(2,1)}), bf16[128,1,16,256]{3,2,1,0:T(8,128)(2,1)S(1)}, u32[]{:S(2)}, u32[]{:S(2)}) async-start(bf16[128,1,16,256]{3,2,1,0:T(8,128)(2,1)} %bitcast.79), calls=%async_computation | async-start | bytes 2097152 | tf_op jit(solution)/shard_map/all_to_all | solution.py:76
  82.5 11.9 %all-to-all-done = bf16[128,1,16,256]{3,2,1,0:T(8,128)(2,1)S(1)} async-done(((bf16[128,1,16,256]{3,2,1,0:T(8,128)(2,1)}), bf16[128,1,16,256]{3,2,1,0:T(8,128)(2,1)S(1)}, u32[]{:S(2)}, u32[]{:S(2)}) %all-to-all-start) | async-done | bytes 1048608 | tf_op jit(solution)/shard_map/all_to_all | solution.py:76
  98.5 41.9 %all-reduce = (f32[]{:T(128)}, f32[]{:T(128)}) all-reduce(f32[]{:T(128)} %get-tuple-element.51, f32[]{:T(128)} %get-tuple-element.50), channel_id=1, replica_groups=mesh['seq'=8,'res'=4] {'seq','res'}, use_global_device_ids=true, to_apply=%region_10.11 | all-reduce | flops 2 | bytes 16 | tf_op jit(solution)/shard_map/psum | solution.py:86
  141.7 1.1 copy.66
  (138 shorter events, 21.6 us)
Async XLA Ops:
  0.6 75.0 %copy-start = (bf16[256,256]{1,0:T(8,128)(2,1)S(1)}, bf16[256,256]{1,0:T(8,128)(2,1)}, u32[]{:S(2)}) copy-start(bf16[256,256]{1,0:T(8,128)(2,1)} %param.13) | copy-start | bytes 393220
  2.5 9.4 %copy-start.2 = (bf16[256,4,256]{2,1,0:T(4,128)(2,1)S(1)}, bf16[256,4,256]{2,1,0:T(4,128)(2,1)}, u32[]{:S(2)}) copy-start(bf16[256,4,256]{2,1,0:T(4,128)(2,1)} %param.12) | copy-start | bytes 1572868
  3.7 8.4 %collective-permute-start = (bf16[16,1,16,256]{3,0,2,1:T(8,128)(2,1)S(1)}, bf16[16,1,16,256]{3,0,2,1:T(8,128)(2,1)S(1)}, u32[]{:S(2)}, u32[]{:S(2)}) collective-permute-start(bf16[16,1,16,256]{3,0,2,1:T(8,128)(2,1)S(1)} %get-tuple-element.68), channel_id=1, source_target_pairs={{0,28},{4,0},{8,4},{12,8},{16,12},{20,16},{24,20},{28,24},{1,29},{... | collective-permute-start | bytes 393224 | tf_op jit(solution)/shard_map/ppermute | solution.py:57
  5.1 20.0 %collective-permute-start.1 = (bf16[16,1,16,256]{3,0,2,1:T(8,128)(2,1)S(1)}, bf16[16,1,16,256]{3,0,2,1:T(8,128)(2,1)S(1)}, u32[]{:S(2)}, u32[]{:S(2)}) collective-permute-start(bf16[16,1,16,256]{3,0,2,1:T(8,128)(2,1)S(1)} %get-tuple-element.67), channel_id=1, source_target_pairs={{0,24},{4,28},{8,0},{12,4},{16,8},{20,12},{24,16},{28,20},{1,25},{... | collective-permute-start | bytes 393224 | tf_op jit(solution)/shard_map/ppermute | solution.py:57
  8.7 18.4 %collective-permute-start.2 = (bf16[16,1,16,256]{3,0,2,1:T(8,128)(2,1)}, bf16[16,1,16,256]{3,0,2,1:T(8,128)(2,1)S(1)}, u32[]{:S(2)}, u32[]{:S(2)}) collective-permute-start(bf16[16,1,16,256]{3,0,2,1:T(8,128)(2,1)} %get-tuple-element.66), channel_id=1, source_target_pairs={{0,20},{4,24},{8,28},{12,0},{16,4},{20,8},{24,12},{28,16},{1,21},{... | collective-permute-start | bytes 393224 | tf_op jit(solution)/shard_map/ppermute | solution.py:57
  8.7 18.4 %collective-permute-start.3 = (bf16[16,1,16,256]{3,0,2,1:T(8,128)(2,1)}, bf16[16,1,16,256]{3,0,2,1:T(8,128)(2,1)S(1)}, u32[]{:S(2)}, u32[]{:S(2)}) collective-permute-start(bf16[16,1,16,256]{3,0,2,1:T(8,128)(2,1)} %get-tuple-element.65), channel_id=1, source_target_pairs={{0,16},{4,20},{8,24},{12,28},{16,0},{20,4},{24,8},{28,12},{1,17},{... | collective-permute-start | bytes 393224 | tf_op jit(solution)/shard_map/ppermute | solution.py:57
  8.7 19.2 %collective-permute-start.4 = (bf16[16,1,16,256]{3,0,2,1:T(8,128)(2,1)S(1)}, bf16[16,1,16,256]{3,0,2,1:T(8,128)(2,1)S(1)}, u32[]{:S(2)}, u32[]{:S(2)}) collective-permute-start(bf16[16,1,16,256]{3,0,2,1:T(8,128)(2,1)S(1)} %get-tuple-element.64), channel_id=1, source_target_pairs={{0,12},{4,16},{8,20},{12,24},{16,28},{20,0},{24,4},{28,8},{1,13},{... | collective-permute-start | bytes 393224 | tf_op jit(solution)/shard_map/ppermute | solution.py:57
  12.1 18.5 %collective-permute-start.5 = (bf16[16,1,16,256]{3,0,2,1:T(8,128)(2,1)S(1)}, bf16[16,1,16,256]{3,0,2,1:T(8,128)(2,1)S(1)}, u32[]{:S(2)}, u32[]{:S(2)}) collective-permute-start(bf16[16,1,16,256]{3,0,2,1:T(8,128)(2,1)S(1)} %get-tuple-element.63), channel_id=1, source_target_pairs={{0,8},{4,12},{8,16},{12,20},{16,24},{20,28},{24,0},{28,4},{1,9},{5... | collective-permute-start | bytes 393224 | tf_op jit(solution)/shard_map/ppermute | solution.py:57
  25.0 5.9 %collective-permute-start.6 = (bf16[16,1,16,256]{3,0,2,1:T(8,128)(2,1)S(1)}, bf16[16,1,16,256]{3,0,2,1:T(8,128)(2,1)S(1)}, u32[]{:S(2)}, u32[]{:S(2)}) collective-permute-start(bf16[16,1,16,256]{3,0,2,1:T(8,128)(2,1)S(1)} %get-tuple-element.62), channel_id=1, source_target_pairs={{0,4},{4,8},{8,12},{12,16},{16,20},{20,24},{24,28},{28,0},{1,5},{5... | collective-permute-start | bytes 393224 | tf_op jit(solution)/shard_map/ppermute | solution.py:57
  31.5 0.9 copy-start.7
  46.4 3.0 %copy-start.1 = (bf16[16,128,256]{2,1,0:T(8,128)(2,1)S(1)}, bf16[16,128,256]{2,1,0:T(8,128)(2,1)}, u32[]{:S(2)}) copy-start(bf16[16,128,256]{2,1,0:T(8,128)(2,1)} %custom-call.1) | copy-start | bytes 3145732
  76.0 5.6 %copy-start.4 = (s32[32,4,16]{0,2,1:T(8,128)S(1)}, s32[32,4,16]{0,2,1:T(8,128)}, u32[]{:S(2)}) copy-start(s32[32,4,16]{0,2,1:T(8,128)} %param.17) | copy-start | bytes 24580
  76.0 5.8 %copy-start.5 = (s32[32,4,16]{0,2,1:T(8,128)S(1)}, s32[32,4,16]{0,2,1:T(8,128)}, u32[]{:S(2)}) copy-start(s32[32,4,16]{0,2,1:T(8,128)} %param.16) | copy-start | bytes 24580
  77.6 16.8 %all-to-all-start = ((bf16[128,1,16,256]{3,2,1,0:T(8,128)(2,1)}), bf16[128,1,16,256]{3,2,1,0:T(8,128)(2,1)S(1)}, u32[]{:S(2)}, u32[]{:S(2)}) async-start(bf16[128,1,16,256]{3,2,1,0:T(8,128)(2,1)} %bitcast.79), calls=%async_computation | async-start | bytes 2097152 | tf_op jit(solution)/shard_map/all_to_all | solution.py:76
  94.8 1.6 %copy-start.8 = (f32[256]{0:T(256)S(1)}, f32[256]{0:T(256)}, u32[]{:S(2)}) copy-start(f32[256]{0:T(256)} %param.14) | copy-start | bytes 3076
  95.3 2.0 %copy-start.6 = (bf16[256,23]{0,1:T(8,128)(2,1)S(1)}, bf16[256,23]{0,1:T(8,128)(2,1)}, u32[]{:S(2)}) copy-start(bf16[256,23]{0,1:T(8,128)(2,1)} %param.15) | copy-start | bytes 35332
  96.4 1.4 copy-start.3
